TPU v7x, 32 devices: a whole 2x2x4 slice. The times are simulated.
32 devices in a mesh: dp: 8 (over z, core), tensor: 4 (over y, x).
Axes of the slice: x: 2, y: 2, z: 4, core: 2. Of those that a mesh axis runs over, the one named last changes fastest.
Arguments:
- block_input: bfloat16 [2048, 5120], P('dp'), may hold values from -6 to 6
- query_weight: bfloat16 [2560, 5120], P('tensor'), as said below
- query_gain: float32 [2560], P('tensor'), may hold values from 0.5 to 2
- query_grad: bfloat16 [2560, 2048], P('tensor', 'dp'), may hold values from -6 to 6
Outputs:
- input_grad: bfloat16 [2048, 5120], P(('dp', 'tensor'))
- weight_grad: float32 [5120, 2560], P('dp', 'tensor')
Inputs may be any that keep to these rules, and one draw needn't show every extreme that they name: `query_weight`: entries are normal with standard deviation 5120 ** -0.5 times a factor between 0.25 and 75, which may differ from row to row and from column to column.
All inputs are finite; a program needn't handle non-finite values.
Results may differ from a plain program's by a relative error of at most 0.017.
Values may be sent and summed in bfloat16 or wider, within the bound.
A program may use at most 64 MiB of HBM per device.

v0:
```python
import jax
import jax.numpy as jnp
from jax import lax
from jax.sharding import PartitionSpec as P

epsilon = 1e-06


def per_device(block_input, query_weight, query_gain, query_grad):
    projected = lax.dot_general(
        query_weight, block_input, (((1,), (1,)), ((), ())), preferred_element_type=jnp.float32
    )
    scaled_grad = query_grad.astype(jnp.float32) * query_gain[:, None]
    squares = jnp.sum(projected * projected, axis=0)
    cross_sums = jnp.sum(scaled_grad * projected, axis=0)
    features = query_gain.shape[0] * lax.axis_size("tensor")
    squares, cross_sums = lax.psum((squares, cross_sums), "tensor")
    inverse_rms = 1.0 / jnp.sqrt(squares / features + epsilon)
    coefficient = inverse_rms * inverse_rms * inverse_rms * (cross_sums / features)
    proj_grad = (inverse_rms[None, :] * scaled_grad - coefficient[None, :] * projected).astype(
        jnp.bfloat16
    )
    columns = proj_grad
    input_grad = lax.psum_scatter(
        lax.dot_general(
            columns, query_weight, (((0,), (0,)), ((), ())), preferred_element_type=jnp.float32
        ).astype(jnp.bfloat16),
        "tensor",
        scatter_dimension=0,
        tiled=True,
    )
    columns = block_input
    weight_grad = lax.psum_scatter(
        lax.dot_general(
            columns, proj_grad, (((0,), (1,)), ((), ())), preferred_element_type=jnp.float32
        ),
        "dp",
        scatter_dimension=0,
        tiled=True,
    )
    return (input_grad, weight_grad)


def solution(mesh):
    in_specs = (P("dp", None), P("tensor", None), P("tensor"), P("tensor", "dp"))
    out_specs = (P(("dp", "tensor"), None), P("dp", "tensor"))
    return jax.shard_map(
        per_device, mesh=mesh, in_specs=in_specs, out_specs=out_specs, check_vma=False
    )
```

profile of v0, /device:TPU:0, one launch (start us, length us, event | category | flops | bytes accessed | tf_op | source)
XLA Modules:
  0.0 215.8 jit_solution(5554739564588748317)
XLA Ops:
  7.2 0.0 copy-start
  7.2 0.0 copy-start.2
  7.2 0.0 copy-start.1
  7.2 0.0 reduce-scatter.5.cloned.1.call-start
  7.2 1.7 copy-done
  8.9 5.6 %multiply_reduce_fusion.1 = (f32[256]{0:T(256)S(1)}, f32[256]{0:T(256)S(1)}, f32[640,256]{1,0:T(8,128)}) fusion(f32[640]{0:T(1024)} %param.6, bf16[640,256]{1,0:T(8,128)(2,1)} %param.7, bf16[640,5120]{1,0:T(8,128)(2,1)} %param.5, bf16[256,5120]{1,0:T(8,128)(2,1)S(1)} %copy-done), kind=kOutput, calls=%fused_computation.5 | convolution fusion | flops 1678704128 | bytes 10162688 | tf_op jit(solution)/shard_map/dot_general | solution.py:10
  14.5 11.4 %all-reduce = (f32[256]{0:T(256)S(1)}, f32[256]{0:T(256)S(1)}) all-reduce(f32[256]{0:T(256)S(1)} %get-tuple-element.5, f32[256]{0:T(256)S(1)} %get-tuple-element.4), channel_id=1, replica_groups=mesh['dp'=8,'tensor'=4] {'tensor'}, use_global_device_ids=true, to_apply=%region_3.0 | all-reduce | flops 512 | bytes 4096 | tf_op jit(solution)/shard_map/psum | solution.py:17
  25.9 0.0 copy-done.2
  25.9 0.0 copy-done.1
  25.9 1.3 subtract_convert_fusion
  27.2 6.5 %convolution_bitcast_fusion = f32[5120,640]{0,1:T(8,128)} fusion(bf16[640,256]{1,0:T(8,128)(2,1)S(1)} %subtract_convert_fusion, bf16[256,5120]{1,0:T(8,128)(2,1)S(1)} %copy-done), kind=kOutput, calls=%fused_computation | convolution fusion | flops 1677721600 | bytes 16056320 | tf_op jit(solution)/shard_map/dot_general | solution.py:34
  33.7 0.0 reduce-scatter.5.cloned.1.call-update
  33.8 0.0 reduce-scatter.3.cloned.1.call-start
  33.8 6.6 %convolution_convert_fusion = bf16[256,5120]{1,0:T(8,128)(2,1)} fusion(bf16[640,256]{1,0:T(8,128)(2,1)S(1)} %subtract_convert_fusion, bf16[640,5120]{1,0:T(8,128)(2,1)} %param.5), kind=kOutput, calls=%fused_computation.1 | convolution fusion | flops 1679032320 | bytes 9502720 | tf_op jit(solution)/shard_map/dot_general | solution.py:25
  40.4 0.0 reduce-scatter.3.cloned.1.call-update
  40.4 127.0 %reduce-scatter.5.cloned.1.call-done = f32[640,640]{0,1:T(8,128)} async-done(((f32[5120,640]{0,1:T(8,128)}), f32[640,640]{0,1:T(8,128)}) %reduce-scatter.5.cloned.1.call-update) | async-done | bytes 1638416 | tf_op jit(solution)/shard_map/reduce_scatter | solution.py:33
  167.4 2.7 %copy.6 = f32[640,640]{1,0:T(8,128)} copy(f32[640,640]{0,1:T(8,128)} %reduce-scatter.5.cloned.1.call-done) | data formatting | bytes 3276800
  170.1 38.9 %reduce-scatter.3.cloned.1.call-done = bf16[64,5120]{1,0:T(8,128)(2,1)} async-done(((bf16[256,5120]{1,0:T(8,128)(2,1)}), bf16[64,5120]{1,0:T(8,128)(2,1)}) %reduce-scatter.3.cloned.1.call-update) | async-done | bytes 655376 | tf_op jit(solution)/shard_map/reduce_scatter | solution.py:24
  (1 shorter events, 0.0 us)
Async XLA Ops:
  7.2 1.7 copy-start
  7.2 18.7 %copy-start.2 = (f32[640]{0:T(1024)S(1)}, f32[640]{0:T(1024)}, u32[]{:S(2)}) copy-start(f32[640]{0:T(1024)} %param.6) | copy-start | bytes 7684
  7.2 18.7 %copy-start.1 = (bf16[640,256]{1,0:T(8,128)(2,1)S(1)}, bf16[640,256]{1,0:T(8,128)(2,1)}, u32[]{:S(2)}) copy-start(bf16[640,256]{1,0:T(8,128)(2,1)} %param.7) | copy-start | bytes 983044
  7.2 160.2 %reduce-scatter.5.cloned.1.call-start = ((), (), s32[]{:S(2)}) async-start(), calls=%async_computation.3 | async-start | bytes 14745600 | tf_op jit(solution)/shard_map/reduce_scatter | solution.py:33
  33.8 175.2 %reduce-scatter.3.cloned.1.call-start = ((), (), s32[]{:S(2)}) async-start(), calls=%async_computation.2 | async-start | bytes 3276800 | tf_op jit(solution)/shard_map/reduce_scatter | solution.py:24
Sparse Core Ops, SparseCore 0:
  33.9 133.4 reduce-scatter.4
  170.9 38.0 reduce-scatter.2
where the time goes:
time: 216 us
  waiting for transfers between devices  166 us (77%)
  matrix products  18.7 us (9%)
  between operations  14.1 us (7%)
  blocking collectives  11.4 us (5%)
  local copies, waits for them, and re-layouts  4.4 us (2%)
    reduce_scatter x1, waiting for transfers between devices, per_device(): lax.psum_scatter(lax.dot_general(columns, proj_grad, (((0,), (1,)), ((),...  127 us
    reduce_scatter x1, waiting for transfers between devices, per_device(): lax.psum_scatter(lax.dot_general(columns, query_weight, (((0,), (0,)), ((...  38.9 us
    psum x1, blocking collectives, per_device(): squares, cross_sums = lax.psum((squares, cross_sums), 'tensor')  11.4 us
    dot_general x1, matrix products, per_device(): lax.dot_general(columns, query_weight, (((0,), (0,)), ((), ())), preferre...  6.57 us
    dot_general x1, matrix products, per_device(): lax.dot_general(columns, proj_grad, (((0,), (1,)), ((), ())), preferred_e...  6.54 us
    dot_general x1, matrix products, per_device(): lax.dot_general(query_weight, block_input, (((1,), (1,)), ((), ())), pref...  5.61 us
    unnamed x7, local copies, waits for them, and re-layouts  4.4 us
  transfers between devices with their start and end apart: 2, of which 2 were waited for; matrix products, arithmetic and copies ran while one was open for 4% of the time, Pallas kernels for 0%

commit v1 on v0

v1 whole, which is shorter than its diff:
```python
import functools

import jax
import jax.numpy as jnp
from jax import lax
from jax.experimental import pallas as pl
from jax.experimental.pallas import tpu as pltpu
from jax.sharding import PartitionSpec as P

epsilon = 1e-06
MESH = pl.DeviceIdType.MESH


def plain(block_input, query_weight, query_gain, query_grad):
    projected = lax.dot_general(
        query_weight, block_input, (((1,), (1,)), ((), ())), preferred_element_type=jnp.float32
    )
    scaled_grad = query_grad.astype(jnp.float32) * query_gain[:, None]
    squares = jnp.sum(projected * projected, axis=0)
    cross_sums = jnp.sum(scaled_grad * projected, axis=0)
    features = query_gain.shape[0] * lax.axis_size("tensor")
    squares, cross_sums = lax.psum((squares, cross_sums), "tensor")
    inverse_rms = 1.0 / jnp.sqrt(squares / features + epsilon)
    coefficient = inverse_rms * inverse_rms * inverse_rms * (cross_sums / features)
    proj_grad = (inverse_rms[None, :] * scaled_grad - coefficient[None, :] * projected).astype(
        jnp.bfloat16
    )
    input_grad = lax.psum_scatter(
        lax.dot_general(
            proj_grad, query_weight, (((0,), (0,)), ((), ())), preferred_element_type=jnp.float32
        ).astype(jnp.bfloat16),
        "tensor",
        scatter_dimension=0,
        tiled=True,
    )
    weight_grad = lax.psum_scatter(
        lax.dot_general(
            block_input, proj_grad, (((0,), (1,)), ((), ())), preferred_element_type=jnp.float32
        ),
        "dp",
        scatter_dimension=0,
        tiled=True,
    )
    return (input_grad, weight_grad)


def kernel(
    ndp, nt, fchunks, nchunks, near,
    x_hbm, w_hbm, qg_hbm, gain_ref,
    ig_ref, wg_ref,
    xv, wv, qv, sg, proj, stats, gt, gbuf, xbuf, part, rsbuf,
    lsem, wsem, st_s, st_r, xs, xr, fs, fr, gs, gr, rs_s, rs_r,
):
    tokens, width = xv.shape
    feats = wv.shape[0]
    cols = width // ndp
    rows = tokens // nt
    fstep = feats // fchunks
    nstep = width // nchunks
    nz = ndp // 2
    d = lax.axis_index("dp")
    t = lax.axis_index("tensor")
    z = d // 2
    c = d % 2
    partner = 2 * z + (1 - c)
    mine = pl.ds(pl.multiple_of(t * rows, rows), rows)

    def remote(src, dst, send, recv, dd, tt):
        return pltpu.make_async_remote_copy(
            src_ref=src, dst_ref=dst, send_sem=send, recv_sem=recv,
            device_id=(dd, tt), device_id_type=MESH,
        )

    x_load = pltpu.make_async_copy(x_hbm, xv, lsem.at[0])
    x_load.start()

    def w_load(i):
        r = pl.ds(i * fstep, fstep)
        return pltpu.make_async_copy(w_hbm.at[r], wv.at[r], wsem.at[i])

    for i in range(fchunks):
        w_load(i).start()
    q_load = pltpu.make_async_copy(qg_hbm, qv, lsem.at[1])
    q_load.start()

    barrier = pltpu.get_barrier_semaphore()
    for o in range(1, ndp):
        pl.semaphore_signal(barrier, inc=1, device_id=((d + o) % ndp, t), device_id_type=MESH)
    for o in range(1, nt):
        pl.semaphore_signal(barrier, inc=1, device_id=(d, (t + o) % nt), device_id_type=MESH)
    pl.semaphore_wait(barrier, ndp + nt - 2)

    def col_block(s):
        return pl.ds(pl.multiple_of(s * cols, cols), cols)

    def x_whole(s, dst_slot, recv_slot):
        return remote(
            x_hbm.at[:, col_block(s)], xbuf.at[dst_slot], xs.at[s], xr.at[recv_slot], s, t
        )

    def x_share(s, dst_slot, recv_slot):
        return remote(
            x_hbm.at[mine, col_block(s)], xbuf.at[dst_slot, mine], xs.at[s], xr.at[recv_slot], s, t
        )

    for zt in range(nz):
        @pl.when(jnp.abs(z - zt) > near)
        def _(zt=zt):
            for ct in range(2):
                x_share(2 * zt + ct, d, d).start()
    x_whole(partner, d, d).start()

    q_load.wait()
    grow = jnp.broadcast_to(gain_ref[...], (128, feats))
    gcol = jnp.transpose(grow)
    for k in range(tokens // 128):
        sl = pl.ds(k * 128, 128)
        sg[:, sl] = qv[:, sl].astype(jnp.float32) * gcol
    x_load.wait()
    sq = jnp.zeros((1, tokens), jnp.float32)
    cr = jnp.zeros((1, tokens), jnp.float32)
    for i in range(fchunks):
        w_load(i).wait()
        r = pl.ds(i * fstep, fstep)
        p = lax.dot_general(
            wv[r, :], xv[...], (((1,), (1,)), ((), ())), preferred_element_type=jnp.float32
        )
        proj[r, :] = p
        sq = sq + jnp.sum(p * p, axis=0, keepdims=True)
        cr = cr + jnp.sum(sg[r, :] * p, axis=0, keepdims=True)
    stats[t, 0:1, :] = sq
    stats[t, 1:2, :] = cr

    def stat_copy(o, slot):
        return remote(stats.at[t], stats.at[slot], st_s.at[o], st_r.at[o], d, (t + o) % nt)

    for o in range(1, nt):
        stat_copy(o, t).start()
    for o in range(1, nt):
        stat_copy(o, (t - o + nt) % nt).wait_recv()
    sq = stats[0, 0:1, :]
    cr = stats[0, 1:2, :]
    for k in range(1, nt):
        sq = sq + stats[k, 0:1, :]
        cr = cr + stats[k, 1:2, :]
    features = feats * nt
    inv = 1.0 / jnp.sqrt(sq / features + epsilon)
    coef = inv * inv * inv * (cr / features)
    gt[...] = inv * sg[...] - coef * proj[...]
    gbuf[d] = jnp.transpose(gt[...]).astype(jnp.bfloat16)

    def g_copy(way, s):
        dd = {0: d - 2, 1: d + 2, 2: partner}[way]
        return remote(gbuf.at[s], gbuf.at[s], gs.at[way, s], gr.at[s], dd, t)

    @pl.when(z > 0)
    def _():
        g_copy(0, d).start()

    @pl.when(z < nz - 1)
    def _():
        g_copy(1, d).start()

    g_copy(2, d).start()

    def x_near(ct):
        for zt in range(nz):
            @pl.when((jnp.abs(z - zt) <= near) & (z != zt))
            def _(zt=zt):
                x_whole(2 * zt + ct, d, d).start()

    x_near(0)

    def rs_copy(n, o, slot, who):
        sl = pl.ds(pl.multiple_of(n * nstep, nstep), nstep)
        rr = pl.ds(pl.multiple_of(who * rows, rows), rows)
        return remote(
            part.at[rr, sl], rsbuf.at[slot, :, sl], rs_s.at[n, o], rs_r.at[n, o], d, who
        )

    def share(n, carry):
        sl = pl.ds(pl.multiple_of(n * nstep, nstep), nstep)
        part[:, sl] = jnp.dot(
            gbuf[d], wv[:, sl], preferred_element_type=jnp.float32
        ).astype(jnp.bfloat16)
        for o in range(1, nt):
            rs_copy(n, o, o, (t + o) % nt).start()
        return carry

    lax.fori_loop(0, nchunks, share, 0)

    def f_copy(s, o):
        return remote(
            xbuf.at[s, mine], xbuf.at[s, mine], fs.at[s, o], fr.at[s, o], d, (t + o) % nt
        )

    def f_arrived(s, o):
        src = (t - o + nt) % nt
        there = pl.ds(pl.multiple_of(src * rows, rows), rows)
        return remote(
            xbuf.at[s, there], xbuf.at[s, there], fs.at[s, o], fr.at[s, o], d, (t + o) % nt
        )

    for dist in range(nz - 1, near, -1):
        for zs_of in (lambda: z - dist, lambda: z + dist):
            zs = zs_of()

            @pl.when((zs >= 0) & (zs < nz))
            def _(zs=zs):
                for cs in range(2):
                    s = 2 * zs + cs
                    x_share(d, s, s).wait_recv()
                    for o in range(1, nt):
                        f_copy(s, o).start()

    def chain(k):
        @pl.when(z - k >= 0)
        def _():
            s = 2 * (z - k) + c
            g_copy(1, s).wait_recv()

            @pl.when(z < nz - 1)
            def _():
                g_copy(1, s).start()

            g_copy(2, s).start()

        @pl.when(z + k < nz)
        def _():
            s = 2 * (z + k) + c
            g_copy(0, s).wait_recv()

            @pl.when(z > 0)
            def _():
                g_copy(0, s).start()

            g_copy(2, s).start()

    def accumulate(s):
        wg_ref[...] += lax.dot_general(
            xbuf[s], gbuf[s], (((0,), (0,)), ((), ())), preferred_element_type=jnp.float32
        )

    def weight_terms(k):
        def one(i, carry):
            zs = z + (2 * (i // 2) - 1) * k
            cs = i % 2

            @pl.when((zs >= 0) & (zs < nz))
            def _():
                s = 2 * zs + cs
                if k <= near:
                    x_whole(d, s, s).wait_recv()
                else:
                    for o in range(1, nt):
                        f_arrived(s, o).wait_recv()

                @pl.when(cs != c)
                def _():
                    g_copy(2, s).wait_recv()

                accumulate(s)

            return carry

        lax.fori_loop(0, 4, one, 0)

    own = pltpu.make_async_copy(x_hbm.at[:, col_block(d)], xbuf.at[d], lsem.at[2])
    own.start()
    chain(1)
    x_near(1)
    own.wait()
    wg_ref[...] = jnp.zeros_like(wg_ref)
    accumulate(d)
    x_whole(d, partner, partner).wait_recv()
    g_copy(2, partner).wait_recv()
    accumulate(partner)
    for k in range(2, nz):
        chain(k)
        weight_terms(k - 1)

    def total(n, carry):
        sl = pl.ds(pl.multiple_of(n * nstep, nstep), nstep)
        acc = part[mine, sl].astype(jnp.float32)
        for o in range(1, nt):
            rs_copy(n, o, o, t).wait_recv()
            acc = acc + rsbuf[o, :, sl].astype(jnp.float32)
        ig_ref[:, sl] = acc.astype(jnp.bfloat16)
        return carry

    lax.fori_loop(0, nchunks, total, 0)
    weight_terms(nz - 1)

    for o in range(1, nt):
        stat_copy(o, t).wait_send()
    for zt in range(nz):
        for ct in range(2):
            s = 2 * zt + ct

            @pl.when(jnp.abs(z - zt) > near)
            def _(s=s):
                x_share(s, d, d).wait_send()
                for o in range(1, nt):
                    f_copy(s, o).wait_send()

            @pl.when((jnp.abs(z - zt) <= near) & (z != zt))
            def _(s=s):
                x_whole(s, d, d).wait_send()

        s = 2 * zt + c

        @pl.when((zt >= z) & (z > 0))
        def _(s=s):
            g_copy(0, s).wait_send()

        @pl.when((zt <= z) & (z < nz - 1))
        def _(s=s):
            g_copy(1, s).wait_send()

        g_copy(2, s).wait_send()
    x_whole(partner, d, d).wait_send()

    def sent(n, carry):
        for o in range(1, nt):
            rs_copy(n, o, o, (t + o) % nt).wait_send()
        return carry

    lax.fori_loop(0, nchunks, sent, 0)


def fused(block_input, query_weight, query_gain, query_grad):
    ndp = lax.axis_size("dp")
    nt = lax.axis_size("tensor")
    tokens, width = block_input.shape
    feats = query_weight.shape[0]
    cols, rows = width // ndp, tokens // nt
    fchunks, nchunks = 2, 4
    dma = pltpu.SemaphoreType.DMA
    bf, f32 = jnp.bfloat16, jnp.float32
    any_spec = pl.BlockSpec(memory_space=pl.ANY)
    vmem = pl.BlockSpec(memory_space=pltpu.VMEM)
    return pl.pallas_call(
        functools.partial(kernel, ndp, nt, fchunks, nchunks, 1),
        out_shape=(
            jax.ShapeDtypeStruct((rows, width), bf),
            jax.ShapeDtypeStruct((cols, feats), f32),
        ),
        in_specs=[any_spec, any_spec, any_spec, vmem],
        out_specs=(vmem, vmem),
        scratch_shapes=[
            pltpu.VMEM((tokens, width), bf),
            pltpu.VMEM((feats, width), bf),
            pltpu.VMEM((feats, tokens), bf),
            pltpu.VMEM((feats, tokens), f32),
            pltpu.VMEM((feats, tokens), f32),
            pltpu.VMEM((nt, 8, tokens), f32),
            pltpu.VMEM((feats, tokens), f32),
            pltpu.VMEM((ndp, tokens, feats), bf),
            pltpu.VMEM((ndp, tokens, cols), bf),
            pltpu.VMEM((tokens, width), bf),
            pltpu.VMEM((nt, rows, width), bf),
            dma((3,)), dma((fchunks,)),
            dma((nt,)), dma((nt,)),
            dma((ndp,)), dma((ndp,)),
            dma((ndp, nt)), dma((ndp, nt)),
            dma((3, ndp)), dma((ndp,)),
            dma((nchunks, nt)), dma((nchunks, nt)),
        ],
        compiler_params=pltpu.CompilerParams(
            collective_id=0, has_side_effects=True, vmem_limit_bytes=56 * 1024 * 1024
        ),
        name="query_backward",
    )(block_input, query_weight, query_grad, query_gain.reshape(1, feats))


def per_device(block_input, query_weight, query_gain, query_grad):
    ndp = lax.axis_size("dp")
    nt = lax.axis_size("tensor")
    tokens, width = block_input.shape
    feats = query_weight.shape[0]
    aligned = (
        ndp % 2 == 0 and ndp >= 4 and nt >= 2
        and width % (128 * ndp) == 0 and width % (128 * 4) == 0
        and feats % 128 == 0 and tokens % 128 == 0 and tokens % (16 * nt) == 0
        and 2 * width * (feats + 4 * tokens) + 24 * tokens * feats < 40 * 2**20
    )
    body = fused if aligned else plain
    return body(block_input, query_weight, query_gain, query_grad)


def solution(mesh):
    in_specs = (P("dp", None), P("tensor", None), P("tensor"), P("tensor", "dp"))
    out_specs = (P(("dp", "tensor"), None), P("dp", "tensor"))
    return jax.shard_map(
        per_device, mesh=mesh, in_specs=in_specs, out_specs=out_specs, check_vma=False
    )
```

time: 216 us -> 69.8 us (0.32)
  waiting for transfers between devices: 166 us -> 0 us
  Pallas kernels: 0 us -> 63 us
  matrix products: 18.7 us -> 0 us
  between operations: 14.1 us -> 0.64 us
  blocking collectives: 11.4 us -> 0 us
    reduce_scatter x2 -> x0, waiting for transfers between devices: 166 us -> none  [the longest x1 127 us: per_device(): lax.psum_scatter(lax.dot_general(columns, proj_grad, (((0,), (1,)), ((),...]
    pallas_call x0 -> x1, Pallas kernels: none -> 63 us  [fused(): pl.pallas_call(functools.partial(kernel, ndp, nt, fchunks, nchunks, 1), o...]
    dot_general x3 -> x0, matrix products: 18.7 us -> none  [the longest x1 6.57 us: per_device(): lax.dot_general(columns, query_weight, (((0,), (0,)), ((), ())), preferre...]
    psum x1 -> x0, blocking collectives: 11.4 us -> none  [per_device(): squares, cross_sums = lax.psum((squares, cross_sums), 'tensor')]
    unnamed x7 -> x2, local copies, waits for them, and re-layouts: 4.4 us -> 4.67 us
  transfers between devices with their start and end apart: 2 -> 0, of which waited for: 2 -> 0; matrix products, arithmetic and copies ran while one was open for 4% -> 0% of each run, Pallas kernels for 0% -> 0%
where the time goes in v1:
time: 69.8 us; the launch traced here: 69.5 us
  Pallas kernels  63 us (90%)
  local copies, waits for them, and re-layouts  5.93 us (8%)
    pallas_call x1, Pallas kernels, fused(): pl.pallas_call(functools.partial(kernel, ndp, nt, fchunks, nchunks, 1), o...  63 us
    unnamed x2, local copies, waits for them, and re-layouts  4.67 us

profile of v1, /device:TPU:0, one launch (start us, length us, event | category | flops | bytes accessed | tf_op | source)
XLA Modules:
  0.0 69.5 jit_solution(1865236867379177487)
XLA Ops:
  0.6 1.3 %reshape.7.gain_ref = f32[1,640]{1,0:T(1,128)} reshape(f32[640]{0:T(1024)} %param.6) | data formatting | bytes 5120 | tf_op jit(solution)/shard_map/reshape | solution.py:373
  1.9 63.0 %query_backward.1 = (bf16[64,5120]{1,0:T(8,128)(2,1)}, f32[640,640]{1,0:T(8,128)}) custom-call(bf16[256,5120]{1,0:T(8,128)(2,1)} %x_hbm.1, bf16[640,5120]{1,0:T(8,128)(2,1)} %w_hbm.1, bf16[640,256]{1,0:T(8,128)(2,1)} %qg_hbm.1, f32[1,640]{1,0:T(1,128)} %reshape.7.gain_ref), custom_call_target="tpu_custom_call" | custom-call | tf_op jit(solution)/shard_map/query_backward/pallas_call | solution.py:342
  64.9 2.0 %copy.8 = bf16[64,5120]{1,0:T(8,128)(2,1)} copy(bf16[64,5120]{1,0:T(8,128)(2,1)} %get-tuple-element.4) | data formatting | bytes 1310720
  66.8 2.7 %copy.9 = f32[640,640]{1,0:T(8,128)} copy(f32[640,640]{1,0:T(8,128)} %get-tuple-element.5) | data formatting | bytes 3276800

commit v2 on v1

--- a/solution.py
+++ b/solution.py
@@ -48,7 +48,7 @@
     ndp, nt, fchunks, nchunks, near,
     x_hbm, w_hbm, qg_hbm, gain_ref,
     ig_ref, wg_ref,
-    xv, wv, qv, sg, proj, stats, gt, gbuf, xbuf, part, rsbuf,
+    xv, wv, qv, sg, proj, stats, gt, gbuf, xbuf, part, rsbuf, relay,
     lsem, wsem, st_s, st_r, xs, xr, fs, fr, gs, gr, rs_s, rs_r,
 ):
     tokens, width = xv.shape
@@ -111,7 +111,7 @@
     x_whole(partner, d, d).start()
 
     q_load.wait()
-    grow = jnp.broadcast_to(gain_ref[...], (128, feats))
+    grow = jnp.broadcast_to(gain_ref[...].reshape(1, feats), (128, feats))
     gcol = jnp.transpose(grow)
     for k in range(tokens // 128):
         sl = pl.ds(k * 128, 128)
@@ -171,35 +171,77 @@
 
     x_near(0)
 
-    def rs_copy(n, o, slot, who):
-        sl = pl.ds(pl.multiple_of(n * nstep, nstep), nstep)
-        rr = pl.ds(pl.multiple_of(who * rows, rows), rows)
+    side = t + 1 - 2 * (t % 2)
+    across = t + 2 - 4 * ((t // 2) % 2)
+
+    def pair(flip):
+        first = side + flip * (across - side)
+        return first, side + across - first
+
+    def run(n):
+        return pl.ds(pl.multiple_of(n * nstep, nstep), nstep)
+
+    def block(who):
+        return pl.ds(pl.multiple_of(who * rows, rows), rows)
+
+    def rs_copy(n, k):
+        first, second = pair(n % 2)
+        src = (
+            part.at[block(side + across - t), run(n)],
+            part.at[block(first), run(n)],
+            relay.at[:, run(n)],
+        )[k]
         return remote(
-            part.at[rr, sl], rsbuf.at[slot, :, sl], rs_s.at[n, o], rs_r.at[n, o], d, who
+            src, rsbuf.at[k, :, run(n)], rs_s.at[n, k], rs_r.at[n, k], d,
+            second if k == 2 else first,
         )
 
     def share(n, carry):
-        sl = pl.ds(pl.multiple_of(n * nstep, nstep), nstep)
-        part[:, sl] = jnp.dot(
-            gbuf[d], wv[:, sl], preferred_element_type=jnp.float32
+        part[:, run(n)] = jnp.dot(
+            gbuf[d], wv[:, run(n)], preferred_element_type=jnp.float32
         ).astype(jnp.bfloat16)
-        for o in range(1, nt):
-            rs_copy(n, o, o, (t + o) % nt).start()
+        rs_copy(n, 0).start()
+        rs_copy(n, 1).start()
         return carry
 
     lax.fori_loop(0, nchunks, share, 0)
 
-    def f_copy(s, o):
+    def pass_on(n, carry):
+        second = pair(n % 2)[1]
+        rs_copy(n, 0).wait_recv()
+        relay[:, run(n)] = (
+            part[block(second), run(n)].astype(jnp.float32)
+            + rsbuf[0, :, run(n)].astype(jnp.float32)
+        ).astype(jnp.bfloat16)
+        rs_copy(n, 2).start()
+        return carry
+
+    def f_copy(s, k, whose=None):
+        cs = s % 2
+        who = (side, across, pair(1 - cs)[0])[k]
+        mine_or = (t, t, pair(cs)[0])[k] if whose is None else whose
         return remote(
-            xbuf.at[s, mine], xbuf.at[s, mine], fs.at[s, o], fr.at[s, o], d, (t + o) % nt
-        )
-
-    def f_arrived(s, o):
-        src = (t - o + nt) % nt
-        there = pl.ds(pl.multiple_of(src * rows, rows), rows)
-        return remote(
-            xbuf.at[s, there], xbuf.at[s, there], fs.at[s, o], fr.at[s, o], d, (t + o) % nt
-        )
+            xbuf.at[s, block(mine_or)], xbuf.at[s, block(mine_or)],
+            fs.at[s, k], fr.at[s, k], d, who,
+        )
+
+    def f_wait(s, k):
+        f_copy(s, k, (side, across, side + across - t)[k]).wait_recv()
+
+    def f_relay(dist):
+        def one(i, carry):
+            zs = z + (2 * (i // 2) - 1) * dist
+
+            @pl.when((zs >= 0) & (zs < nz))
+            def _():
+                s = 2 * zs + i % 2
+                f_wait(s, 0)
+                f_wait(s, 1)
+                f_copy(s, 2).start()
+
+            return carry
+
+        lax.fori_loop(0, 4, one, 0)
 
     for dist in range(nz - 1, near, -1):
         for zs_of in (lambda: z - dist, lambda: z + dist):
@@ -210,8 +252,8 @@
                 for cs in range(2):
                     s = 2 * zs + cs
                     x_share(d, s, s).wait_recv()
-                    for o in range(1, nt):
-                        f_copy(s, o).start()
+                    f_copy(s, 0).start()
+                    f_copy(s, 1).start()
 
     def chain(k):
         @pl.when(z - k >= 0)
@@ -252,8 +294,7 @@
                 if k <= near:
                     x_whole(d, s, s).wait_recv()
                 else:
-                    for o in range(1, nt):
-                        f_arrived(s, o).wait_recv()
+                    f_wait(s, 2)
 
                 @pl.when(cs != c)
                 def _():
@@ -268,6 +309,7 @@
     own = pltpu.make_async_copy(x_hbm.at[:, col_block(d)], xbuf.at[d], lsem.at[2])
     own.start()
     chain(1)
+    lax.fori_loop(0, nchunks // 2, pass_on, 0)
     x_near(1)
     own.wait()
     wg_ref[...] = jnp.zeros_like(wg_ref)
@@ -275,17 +317,21 @@
     x_whole(d, partner, partner).wait_recv()
     g_copy(2, partner).wait_recv()
     accumulate(partner)
+    lax.fori_loop(nchunks // 2, nchunks, pass_on, 0)
     for k in range(2, nz):
         chain(k)
+        for dist in range(nz - 1, near, -1):
+            if k == 2:
+                f_relay(dist)
         weight_terms(k - 1)
 
     def total(n, carry):
-        sl = pl.ds(pl.multiple_of(n * nstep, nstep), nstep)
-        acc = part[mine, sl].astype(jnp.float32)
-        for o in range(1, nt):
-            rs_copy(n, o, o, t).wait_recv()
-            acc = acc + rsbuf[o, :, sl].astype(jnp.float32)
-        ig_ref[:, sl] = acc.astype(jnp.bfloat16)
+        rs_copy(n, 1).wait_recv()
+        rs_copy(n, 2).wait_recv()
+        acc = part[mine, run(n)].astype(jnp.float32)
+        for k in (1, 2):
+            acc = acc + rsbuf[k, :, run(n)].astype(jnp.float32)
+        ig_ref[:, run(n)] = acc.astype(jnp.bfloat16)
         return carry
 
     lax.fori_loop(0, nchunks, total, 0)
@@ -300,8 +346,8 @@
             @pl.when(jnp.abs(z - zt) > near)
             def _(s=s):
                 x_share(s, d, d).wait_send()
-                for o in range(1, nt):
-                    f_copy(s, o).wait_send()
+                for k in range(3):
+                    f_copy(s, k).wait_send()
 
             @pl.when((jnp.abs(z - zt) <= near) & (z != zt))
             def _(s=s):
@@ -321,11 +367,22 @@
     x_whole(partner, d, d).wait_send()
 
     def sent(n, carry):
-        for o in range(1, nt):
-            rs_copy(n, o, o, (t + o) % nt).wait_send()
+        for k in range(3):
+            rs_copy(n, k).wait_send()
         return carry
 
     lax.fori_loop(0, nchunks, sent, 0)
+
+
+def write_out(ig_ref, wg_ref, ig_hbm, wg_hbm, sem):
+    copies = (
+        pltpu.make_async_copy(ig_ref, ig_hbm, sem.at[0]),
+        pltpu.make_async_copy(wg_ref, wg_hbm, sem.at[1]),
+    )
+    for copy in copies:
+        copy.start()
+    for copy in copies:
+        copy.wait()
 
 
 def fused(block_input, query_weight, query_gain, query_grad):
@@ -337,15 +394,15 @@
     fchunks, nchunks = 2, 4
     dma = pltpu.SemaphoreType.DMA
     bf, f32 = jnp.bfloat16, jnp.float32
-    any_spec = pl.BlockSpec(memory_space=pl.ANY)
+    hbm = pl.BlockSpec(memory_space=pltpu.HBM)
     vmem = pl.BlockSpec(memory_space=pltpu.VMEM)
-    return pl.pallas_call(
+    outs = pl.pallas_call(
         functools.partial(kernel, ndp, nt, fchunks, nchunks, 1),
         out_shape=(
-            jax.ShapeDtypeStruct((rows, width), bf),
-            jax.ShapeDtypeStruct((cols, feats), f32),
+            pltpu.VMEM((rows, width), bf),
+            pltpu.VMEM((cols, feats), f32),
         ),
-        in_specs=[any_spec, any_spec, any_spec, vmem],
+        in_specs=[hbm, hbm, hbm, vmem],
         out_specs=(vmem, vmem),
         scratch_shapes=[
             pltpu.VMEM((tokens, width), bf),
@@ -358,19 +415,29 @@
             pltpu.VMEM((ndp, tokens, feats), bf),
             pltpu.VMEM((ndp, tokens, cols), bf),
             pltpu.VMEM((tokens, width), bf),
-            pltpu.VMEM((nt, rows, width), bf),
+            pltpu.VMEM((3, rows, width), bf),
+            pltpu.VMEM((rows, width), bf),
             dma((3,)), dma((fchunks,)),
             dma((nt,)), dma((nt,)),
             dma((ndp,)), dma((ndp,)),
-            dma((ndp, nt)), dma((ndp, nt)),
+            dma((ndp, 3)), dma((ndp, 3)),
             dma((3, ndp)), dma((ndp,)),
-            dma((nchunks, nt)), dma((nchunks, nt)),
+            dma((nchunks, 3)), dma((nchunks, 3)),
         ],
         compiler_params=pltpu.CompilerParams(
-            collective_id=0, has_side_effects=True, vmem_limit_bytes=56 * 1024 * 1024
+            collective_id=0, has_side_effects=True, vmem_limit_bytes=64 * 1024 * 1024 - 2560 * 1024
         ),
         name="query_backward",
-    )(block_input, query_weight, query_grad, query_gain.reshape(1, feats))
+    )(block_input, query_weight, query_grad, query_gain)
+    return pl.pallas_call(
+        write_out,
+        out_shape=tuple(jax.ShapeDtypeStruct(o.shape, o.dtype) for o in outs),
+        in_specs=[vmem, vmem],
+        out_specs=(hbm, hbm),
+        scratch_shapes=[dma((2,))],
+        compiler_params=pltpu.CompilerParams(vmem_limit_bytes=8 * 1024 * 1024),
+        name="write_out",
+    )(*outs)
 
 
 def per_device(block_input, query_weight, query_gain, query_grad):
@@ -379,7 +446,7 @@
     tokens, width = block_input.shape
     feats = query_weight.shape[0]
     aligned = (
-        ndp % 2 == 0 and ndp >= 4 and nt >= 2
+        ndp % 2 == 0 and ndp >= 6 and nt == 4
         and width % (128 * ndp) == 0 and width % (128 * 4) == 0
         and feats % 128 == 0 and tokens % 128 == 0 and tokens % (16 * nt) == 0
         and 2 * width * (feats + 4 * tokens) + 24 * tokens * feats < 40 * 2**20

time: 69.8 us -> 59 us (0.85)
  local copies, waits for them, and re-layouts: 5.93 us -> 0 us
  Pallas kernels: 63 us -> 58.2 us
    pallas_call x1, Pallas kernels: 63 us -> 56.8 us  [fused(): pl.pallas_call(functools.partial(kernel, ndp, nt, fchunks, nchunks, 1), o...]
    unnamed x2 -> x0, local copies, waits for them, and re-layouts: 4.67 us -> none
    pallas_call x0 -> x1, Pallas kernels: none -> 1.4 us  [fused(): pl.pallas_call(write_out, out_shape=tuple((jax.ShapeDtypeStruct(o.shape,...]
    reshape x1 -> x0, local copies, waits for them, and re-layouts: 1.27 us -> none  [fused(): query_gain.reshape(1, feats)]
where the time goes in v2:
time: 59 us; the launch traced here: 58.8 us
  Pallas kernels  58.2 us (99%)
  between operations  0.64 us (1%)
    pallas_call x1, Pallas kernels, fused(): pl.pallas_call(functools.partial(kernel, ndp, nt, fchunks, nchunks, 1), o...  56.8 us
    pallas_call x1, Pallas kernels, fused(): pl.pallas_call(write_out, out_shape=tuple((jax.ShapeDtypeStruct(o.shape,...  1.4 us

profile of v2, /device:TPU:0, one launch (start us, length us, event | category | flops | bytes accessed | tf_op | source)
XLA Modules:
  0.0 58.8 jit_solution(10150555908554432966)
XLA Ops:
  0.6 56.8 %query_backward.1 = (bf16[64,5120]{1,0:T(8,128)(2,1)S(1)}, f32[640,640]{1,0:T(8,128)S(1)}) custom-call(bf16[256,5120]{1,0:T(8,128)(2,1)} %x_hbm.1, bf16[640,5120]{1,0:T(8,128)(2,1)} %w_hbm.1, bf16[640,256]{1,0:T(8,128)(2,1)} %qg_hbm.1, f32[640]{0:T(1024)} %gain_ref.1), custom_call_target="tpu_custom_call" | custom-call | tf_op jit(solution)/shard_map/query_backward/pallas_call | solution.py:399
  57.4 1.4 %write_out.1 = (bf16[64,5120]{1,0:T(8,128)(2,1)}, f32[640,640]{1,0:T(8,128)}) custom-call(bf16[64,5120]{1,0:T(8,128)(2,1)S(1)} %get-tuple-element.4.ig_ref, f32[640,640]{1,0:T(8,128)S(1)} %get-tuple-element.5.wg_ref), custom_call_target="tpu_custom_call" | custom-call | tf_op jit(solution)/shard_map/write_out/pallas_call | solution.py:432
